TPU v7x, 128 devices: a whole 4x4x4 slice. The times are simulated.
128 devices in a mesh: rep: 16 (over x, z_lo, core), tp: 8 (over z_hi, y).
Axes of the slice: x: 4, y: 4, z: 4 (z_hi: 2, z_lo: 2; z = z_hi * 2 + z_lo), core: 2. Of those that a mesh axis runs over, the one named last changes fastest.
Arguments:
- flat_buffer: bfloat16 [579207168], P(('rep', 'tp')), may hold values from -60 to 60
- shard_pad: int32 [2, 6], replicated, may hold values from 0 to 2
Outputs:
- q_served: bfloat16 [2, 6144, 6144], P(None, 'rep', 'tp')
- q_scale: float32 [2, 48, 6144], P(None, 'rep', 'tp')
- k_served: bfloat16 [2, 6144, 1024], P(None, 'rep', 'tp')
- k_scale: float32 [2, 48, 1024], P(None, 'rep', 'tp')
- v_served: bfloat16 [2, 6144, 1024], P(None, 'rep', 'tp')
- v_scale: float32 [2, 48, 1024], P(None, 'rep', 'tp')
- o_served: bfloat16 [2, 6144, 6144], P(None, 'tp', 'rep')
- o_scale: float32 [2, 48, 6144], P(None, 'tp', 'rep')
- gate_served: bfloat16 [2, 6144, 16384], P(None, 'rep', 'tp')
- gate_scale: float32 [2, 48, 16384], P(None, 'rep', 'tp')
- up_served: bfloat16 [2, 6144, 16384], P(None, 'rep', 'tp')
- up_scale: float32 [2, 48, 16384], P(None, 'rep', 'tp')
All inputs are finite; a program needn't handle non-finite values. Where the computation divides by a largest or mean magnitude, that divisor is 1e-20 or more.
Results may differ from a plain program's by a relative error of at most 0.001.
Values may be sent and summed in bfloat16 or wider, within the bound.
A program may use at most 128 MiB of HBM per device.

v0:
```python
import jax.numpy as jnp
from jax import lax

DEVICES = 128
D = 6144
KV = 1024
FF = 16384
GROUP = 128
LAYERS = 2
FLAT_DEV = 4525056


def quantize(served):
    values = served.astype(jnp.float32)
    grouped = values.reshape(values.shape[0] // GROUP, GROUP, values.shape[1])
    peak = jnp.max(jnp.abs(grouped), axis=1) + 1e-06
    scaled = (grouped / peak[:, None, :]).astype(jnp.bfloat16)
    return (scaled.reshape(served.shape), peak)


def reference(flat_buffer, shard_pad):
    widths = (D, KV, KV, D, FF, FF)
    table = flat_buffer.reshape(DEVICES, FLAT_DEV)
    offset = jnp.zeros((), jnp.int32)
    served_all = [[] for index in range(6)]
    scale_all = [[] for index in range(6)]
    for layer in range(LAYERS):
        for index in range(6):
            length = widths[index] // DEVICES * D
            piece = lax.dynamic_slice_in_dim(table, offset.astype(jnp.int32), length, 1)
            whole = piece.reshape(widths[index], D)
            scaled, peak = quantize(whole.T)
            served_all[index].append(scaled)
            scale_all[index].append(peak)
            offset = (offset + length + 128 * shard_pad[layer, index]).astype(jnp.int32)
    outputs = []
    for index in range(6):
        outputs.append(jnp.stack(served_all[index]))
        outputs.append(jnp.stack(scale_all[index]))
    return (
        outputs[0],
        outputs[1],
        outputs[2],
        outputs[3],
        outputs[4],
        outputs[5],
        outputs[6],
        outputs[7],
        outputs[8],
        outputs[9],
        outputs[10],
        outputs[11],
    )


def solution(mesh):
    return reference
```

profile of v0, /device:TPU:96, one launch (start us, length us, event | category | flops | bytes accessed | tf_op | source)
XLA Modules:
  0.0 650.0 jit_solution(4623308103086450527)
XLA Ops:
  11.8 5.8 all-to-all-start.6
  19.6 109.2 %while = (u32[]{:T(128)}, bf16[4525056]{0:T(1024)(128)(2,1)}, bf16[1,1,4525056]{2,1,0:T(2,128)(2,1)}) while((u32[]{:T(128)}, bf16[4525056]{0:T(1024)(128)(2,1)}, bf16[1,1,4525056]{2,1,0:T(2,128)(2,1)}) %tuple.52), condition=%cond, body=%body | while | flops 9 | bytes 36200596
  24.7 104.1 %reshape_dynamic-update-slice_fusion = bf16[1,1,4525056]{2,1,0:T(2,128)(2,1)} fusion(bf16[1,1,4525056]{2,1,0:T(2,128)(2,1)} %get-tuple-element.149, u32[]{:T(128)S(6)} %multiply.89, u32[]{:T(128)S(6)} %multiply.90, bf16[4525056]{0:T(1024)(128)(2,1)S(1)} %dynamic-slice.122), kind=kLoop, calls=%fused_computation.110 | loop fusion | bytes 18100232
  128.8 11.2 %fusion.16 = f32[294912]{0:T(1024)S(1)} fusion(bf16[1,4525056]{1,0:T(2,128)(2,1)} %bitcast.475), kind=kLoop, calls=%fused_computation.35 | loop fusion | flops 294912 | bytes 1769472 | tf_op jit(solution)/convert_element_type | solution.py:14
  155.4 10.6 %dynamic-slice_convert_fusion.1 = (f32[786432]{0:T(1024)}, f32[786432]{0:T(1024)}, f32[786432]{0:T(1024)}, f32[786432]{0:T(1024)}) fusion(bf16[4525056]{0:T(1024)(128)(2,1)} %get-tuple-element.153, s32[]{:T(128)S(6)} %select_n.42, s32[]{:T(128)S(6)} %select_n.43, s32[]{:T(128)S(6)} %select_n.41, s32[]{:T(128)S(6)} %select_n.40), kind=kLoop, calls=%fused_computation.19 | loop fusion | flops 3145728 | bytes 18874384 | tf_op jit(solution)/convert_element_type | solution.py:14
  207.0 5.7 all-to-all-start.10
  218.9 7.4 %all-to-all-start.7 = ((f32[2,3,8,2,1,8]{5,3,1,0,4,2:T(2,128)}), f32[2,3,8,2,1,8]{5,3,1,0,4,2:T(2,128)S(1)}, u32[]{:S(2)}, u32[]{:S(2)}) async-start(f32[2,3,8,2,1,8]{5,3,1,0,4,2:T(2,128)} %copy.261), calls=%async_computation.7 | async-start | bytes 98304 | tf_op jit(solution)/call_exported;jit(solution)/stack
  231.2 6.2 all-to-all-start.11
  242.2 5.7 all-to-all-start.2
  256.4 6.8 %all-to-all-start.13 = ((f32[8,1,576]{2,1,0:T(1,128)}), f32[8,1,576]{2,1,0:T(1,128)}, u32[]{:S(2)}, u32[]{:S(2)}) async-start(f32[8,1,576]{2,1,0:T(1,128)} %reshape.610), calls=%async_computation.13 | async-start | bytes 40960 | tf_op jit(solution)/call_exported;jit(solution)/stack
  271.7 7.2 %all-to-all-start.3 = ((f32[8,1,576]{2,1,0:T(1,128)}), f32[8,1,576]{2,1,0:T(1,128)}, u32[]{:S(2)}, u32[]{:S(2)}) async-start(f32[8,1,576]{2,1,0:T(1,128)} %reshape.608), calls=%async_computation.3 | async-start | bytes 40960 | tf_op jit(solution)/call_exported;jit(solution)/stack
  304.7 6.1 all-to-all-start.17
  315.7 6.3 all-to-all-start.21
  347.6 6.9 %all-to-all-start.5 = ((bf16[2,384,8,2,1,8]{1,5,3,0,4,2:T(8,128)(2,1)}), bf16[2,384,8,2,1,8]{1,5,3,0,4,2:T(8,128)(2,1)S(1)}, u32[]{:S(2)}, u32[]{:S(2)}) async-start(bf16[2,384,8,2,1,8]{1,5,3,0,4,2:T(8,128)(2,1)} %copy.256), calls=%async_computation.5 | async-start | bytes 393216 | tf_op jit(solution)/call_exported;jit(solution)/stack
  360.5 6.3 all-to-all-start.9
  382.5 11.4 %all-to-all-done = bf16[2,16,384,1,1,48]{2,5,0,4,3,1:T(8,128)(2,1)} async-done(((bf16[2,16,384,1,1,48]{2,5,0,4,3,1:T(8,128)(2,1)}), bf16[2,16,384,1,1,48]{2,5,0,4,3,1:T(8,128)(2,1)}, u32[]{:S(2)}, u32[]{:S(2)}) %all-to-all-start) | async-done | bytes 1179680 | tf_op jit(solution)/call_exported;jit(solution)/stack
  393.9 7.7 %all-to-all-start.12 = ((bf16[2,8,768,1,48]{2,4,0,3,1:T(8,128)(2,1)}), bf16[2,8,768,1,48]{2,4,0,3,1:T(8,128)(2,1)}, u32[]{:S(2)}, u32[]{:S(2)}) async-start(bf16[2,8,768,1,48]{2,4,0,3,1:T(8,128)(2,1)} %copy.272), calls=%async_computation.12 | async-start | bytes 2359296 | tf_op jit(solution)/call_exported;jit(solution)/stack
  404.2 14.0 %all-to-all-done.12 = bf16[2,8,768,1,48]{2,4,0,3,1:T(8,128)(2,1)} async-done(((bf16[2,8,768,1,48]{2,4,0,3,1:T(8,128)(2,1)}), bf16[2,8,768,1,48]{2,4,0,3,1:T(8,128)(2,1)}, u32[]{:S(2)}, u32[]{:S(2)}) %all-to-all-start.12) | async-done | bytes 1179680 | tf_op jit(solution)/call_exported;jit(solution)/stack
  418.2 7.1 %all-to-all-start.1 = ((bf16[2,384,8,2,1,48]{1,5,3,0,4,2:T(8,128)(2,1)}), bf16[2,384,8,2,1,48]{1,5,3,0,4,2:T(8,128)(2,1)}, u32[]{:S(2)}, u32[]{:S(2)}) async-start(bf16[2,384,8,2,1,48]{1,5,3,0,4,2:T(8,128)(2,1)} %copy.247), calls=%async_computation.1 | async-start | bytes 2359296 | tf_op jit(solution)/call_exported;jit(solution)/stack
  456.9 32.0 %all-to-all-done.14 = bf16[2,16,384,1,1,128]{5,2,0,4,3,1:T(8,128)(2,1)} async-done(((bf16[2,16,384,1,1,128]{5,2,0,4,3,1:T(8,128)(2,1)}), bf16[2,16,384,1,1,128]{5,2,0,4,3,1:T(8,128)(2,1)}, u32[]{:S(2)}, u32[]{:S(2)}) %all-to-all-start.14) | async-done | bytes 3145760 | tf_op jit(solution)/call_exported;jit(solution)/stack
  498.5 38.3 %all-to-all-done.18 = bf16[2,16,384,1,1,128]{5,2,0,4,3,1:T(8,128)(2,1)S(1)} async-done(((bf16[2,16,384,1,1,128]{5,2,0,4,3,1:T(8,128)(2,1)}), bf16[2,16,384,1,1,128]{5,2,0,4,3,1:T(8,128)(2,1)S(1)}, u32[]{:S(2)}, u32[]{:S(2)}) %all-to-all-start.18) | async-done | bytes 3145760 | tf_op jit(solution)/call_exported;jit(solution)/stack
  538.4 6.3 all-to-all-start.15
  548.9 33.3 %all-to-all-done.15 = bf16[2,384,8,2,1,128]{5,1,3,0,4,2:T(8,128)(2,1)S(1)} async-done(((bf16[2,384,8,2,1,128]{5,1,3,0,4,2:T(8,128)(2,1)}), bf16[2,384,8,2,1,128]{5,1,3,0,4,2:T(8,128)(2,1)S(1)}, u32[]{:S(2)}, u32[]{:S(2)}) %all-to-all-start.15) | async-done | bytes 3145760 | tf_op jit(solution)/call_exported;jit(solution)/stack
  582.2 16.5 %all-to-all-start.19 = ((bf16[2,384,8,2,1,128]{5,1,3,0,4,2:T(8,128)(2,1)}), bf16[2,384,8,2,1,128]{5,1,3,0,4,2:T(8,128)(2,1)}, u32[]{:S(2)}, u32[]{:S(2)}) async-start(bf16[2,384,8,2,1,128]{5,1,3,0,4,2:T(8,128)(2,1)} %copy.288), calls=%async_computation.19 | async-start | bytes 6291456 | tf_op jit(solution)/call_exported;jit(solution)/stack
  (241 shorter events, 277.9 us)
Async XLA Ops:
  11.8 195.1 %all-to-all-start.6 = ((f32[2,16,3,1,1,8]{5,0,2,4,3,1:T(2,128)}), f32[2,16,3,1,1,8]{5,0,2,4,3,1:T(2,128)}, u32[]{:S(2)}, u32[]{:S(2)}) async-start(f32[2,16,3,1,1,8]{5,0,2,4,3,1:T(2,128)} %bitcast.39), calls=%async_computation.6 | async-start | bytes 98304 | tf_op jit(solution)/call_exported;jit(solution)/stack
  207.0 11.9 %all-to-all-start.10 = ((f32[2,16,3,1,1,8]{5,0,2,4,3,1:T(2,128)}), f32[2,16,3,1,1,8]{5,0,2,4,3,1:T(2,128)S(1)}, u32[]{:S(2)}, u32[]{:S(2)}) async-start(f32[2,16,3,1,1,8]{5,0,2,4,3,1:T(2,128)} %bitcast.60), calls=%async_computation.10 | async-start | bytes 98304 | tf_op jit(solution)/call_exported;jit(solution)/stack
  218.9 12.3 %all-to-all-start.7 = ((f32[2,3,8,2,1,8]{5,3,1,0,4,2:T(2,128)}), f32[2,3,8,2,1,8]{5,3,1,0,4,2:T(2,128)S(1)}, u32[]{:S(2)}, u32[]{:S(2)}) async-start(f32[2,3,8,2,1,8]{5,3,1,0,4,2:T(2,128)} %copy.261), calls=%async_computation.7 | async-start | bytes 98304 | tf_op jit(solution)/call_exported;jit(solution)/stack
  231.2 11.1 %all-to-all-start.11 = ((f32[2,3,8,2,1,8]{5,3,1,0,4,2:T(2,128)}), f32[2,3,8,2,1,8]{5,3,1,0,4,2:T(2,128)S(1)}, u32[]{:S(2)}, u32[]{:S(2)}) async-start(f32[2,3,8,2,1,8]{5,3,1,0,4,2:T(2,128)} %copy.270), calls=%async_computation.11 | async-start | bytes 98304 | tf_op jit(solution)/call_exported;jit(solution)/stack
  242.2 14.1 %all-to-all-start.2 = ((f32[16,1,288]{2,1,0:T(1,128)}), f32[16,1,288]{2,1,0:T(1,128)}, u32[]{:S(2)}, u32[]{:S(2)}) async-start(f32[16,1,288]{2,1,0:T(1,128)} %reshape.606), calls=%async_computation.2 | async-start | bytes 49152 | tf_op jit(solution)/call_exported;jit(solution)/stack
  252.9 46.8 %copy-start.16 = (f32[8,6144]{1,0:T(8,128)S(1)}, f32[8,6144]{1,0:T(8,128)}, u32[]{:S(2)}) copy-start(f32[8,6144]{1,0:T(8,128)} %copy-done.15) | copy-start | bytes 589828
  252.9 46.8 %copy-start.18 = (f32[8,6144]{1,0:T(8,128)S(1)}, f32[8,6144]{1,0:T(8,128)}, u32[]{:S(2)}) copy-start(f32[8,6144]{1,0:T(8,128)} %copy-done.17) | copy-start | bytes 589828
  256.4 15.3 %all-to-all-start.13 = ((f32[8,1,576]{2,1,0:T(1,128)}), f32[8,1,576]{2,1,0:T(1,128)}, u32[]{:S(2)}, u32[]{:S(2)}) async-start(f32[8,1,576]{2,1,0:T(1,128)} %reshape.610), calls=%async_computation.13 | async-start | bytes 40960 | tf_op jit(solution)/call_exported;jit(solution)/stack
  271.7 12.1 %all-to-all-start.3 = ((f32[8,1,576]{2,1,0:T(1,128)}), f32[8,1,576]{2,1,0:T(1,128)}, u32[]{:S(2)}, u32[]{:S(2)}) async-start(f32[8,1,576]{2,1,0:T(1,128)} %reshape.608), calls=%async_computation.3 | async-start | bytes 40960 | tf_op jit(solution)/call_exported;jit(solution)/stack
  283.8 10.7 %all-to-all-start.16 = ((f32[2,16,3,1,1,128]{5,0,2,4,3,1:T(2,128)}), f32[2,16,3,1,1,128]{5,0,2,4,3,1:T(2,128)}, u32[]{:S(2)}, u32[]{:S(2)}) async-start(f32[2,16,3,1,1,128]{5,0,2,4,3,1:T(2,128)} %bitcast.474), calls=%async_computation.16 | async-start | bytes 98304 | tf_op jit(solution)/call_exported;jit(solution)/stack
  294.5 10.3 %all-to-all-start.20 = ((f32[2,16,3,1,1,128]{5,0,2,4,3,1:T(2,128)}), f32[2,16,3,1,1,128]{5,0,2,4,3,1:T(2,128)}, u32[]{:S(2)}, u32[]{:S(2)}) async-start(f32[2,16,3,1,1,128]{5,0,2,4,3,1:T(2,128)} %bitcast.473), calls=%async_computation.20 | async-start | bytes 98304 | tf_op jit(solution)/call_exported;jit(solution)/stack
  304.7 10.9 %all-to-all-start.17 = ((f32[2,3,8,2,1,128]{5,3,1,0,4,2:T(2,128)}), f32[2,3,8,2,1,128]{5,3,1,0,4,2:T(2,128)S(1)}, u32[]{:S(2)}, u32[]{:S(2)}) async-start(f32[2,3,8,2,1,128]{5,3,1,0,4,2:T(2,128)} %copy.284), calls=%async_computation.17 | async-start | bytes 98304 | tf_op jit(solution)/call_exported;jit(solution)/stack
  315.7 11.1 %all-to-all-start.21 = ((f32[2,3,8,2,1,128]{5,3,1,0,4,2:T(2,128)}), f32[2,3,8,2,1,128]{5,3,1,0,4,2:T(2,128)S(1)}, u32[]{:S(2)}, u32[]{:S(2)}) async-start(f32[2,3,8,2,1,128]{5,3,1,0,4,2:T(2,128)} %copy.293), calls=%async_computation.21 | async-start | bytes 98304 | tf_op jit(solution)/call_exported;jit(solution)/stack
  327.4 9.7 %all-to-all-start.4 = ((bf16[2,16,384,1,1,8]{2,5,0,4,3,1:T(8,128)(2,1)}), bf16[2,16,384,1,1,8]{2,5,0,4,3,1:T(8,128)(2,1)S(1)}, u32[]{:S(2)}, u32[]{:S(2)}) async-start(bf16[2,16,384,1,1,8]{2,5,0,4,3,1:T(8,128)(2,1)} %copy.254), calls=%async_computation.4 | async-start | bytes 393216 | tf_op jit(solution)/call_exported;jit(solution)/stack
  337.1 10.6 %all-to-all-start.8 = ((bf16[2,16,384,1,1,8]{2,5,0,4,3,1:T(8,128)(2,1)}), bf16[2,16,384,1,1,8]{2,5,0,4,3,1:T(8,128)(2,1)S(1)}, u32[]{:S(2)}, u32[]{:S(2)}) async-start(bf16[2,16,384,1,1,8]{2,5,0,4,3,1:T(8,128)(2,1)} %copy.263), calls=%async_computation.8 | async-start | bytes 393216 | tf_op jit(solution)/call_exported;jit(solution)/stack
  347.6 12.8 %all-to-all-start.5 = ((bf16[2,384,8,2,1,8]{1,5,3,0,4,2:T(8,128)(2,1)}), bf16[2,384,8,2,1,8]{1,5,3,0,4,2:T(8,128)(2,1)S(1)}, u32[]{:S(2)}, u32[]{:S(2)}) async-start(bf16[2,384,8,2,1,8]{1,5,3,0,4,2:T(8,128)(2,1)} %copy.256), calls=%async_computation.5 | async-start | bytes 393216 | tf_op jit(solution)/call_exported;jit(solution)/stack
  360.5 11.8 %all-to-all-start.9 = ((bf16[2,384,8,2,1,8]{1,5,3,0,4,2:T(8,128)(2,1)}), bf16[2,384,8,2,1,8]{1,5,3,0,4,2:T(8,128)(2,1)S(1)}, u32[]{:S(2)}, u32[]{:S(2)}) async-start(bf16[2,384,8,2,1,8]{1,5,3,0,4,2:T(8,128)(2,1)} %copy.265), calls=%async_computation.9 | async-start | bytes 393216 | tf_op jit(solution)/call_exported;jit(solution)/stack
  372.2 21.7 %all-to-all-start = ((bf16[2,16,384,1,1,48]{2,5,0,4,3,1:T(8,128)(2,1)}), bf16[2,16,384,1,1,48]{2,5,0,4,3,1:T(8,128)(2,1)}, u32[]{:S(2)}, u32[]{:S(2)}) async-start(bf16[2,16,384,1,1,48]{2,5,0,4,3,1:T(8,128)(2,1)} %copy.245), calls=%async_computation | async-start | bytes 2359296 | tf_op jit(solution)/call_exported;jit(solution)/stack
  393.9 24.3 %all-to-all-start.12 = ((bf16[2,8,768,1,48]{2,4,0,3,1:T(8,128)(2,1)}), bf16[2,8,768,1,48]{2,4,0,3,1:T(8,128)(2,1)}, u32[]{:S(2)}, u32[]{:S(2)}) async-start(bf16[2,8,768,1,48]{2,4,0,3,1:T(8,128)(2,1)} %copy.272), calls=%async_computation.12 | async-start | bytes 2359296 | tf_op jit(solution)/call_exported;jit(solution)/stack
  418.2 23.1 %all-to-all-start.1 = ((bf16[2,384,8,2,1,48]{1,5,3,0,4,2:T(8,128)(2,1)}), bf16[2,384,8,2,1,48]{1,5,3,0,4,2:T(8,128)(2,1)}, u32[]{:S(2)}, u32[]{:S(2)}) async-start(bf16[2,384,8,2,1,48]{1,5,3,0,4,2:T(8,128)(2,1)} %copy.247), calls=%async_computation.1 | async-start | bytes 2359296 | tf_op jit(solution)/call_exported;jit(solution)/stack
  441.3 47.6 %all-to-all-start.14 = ((bf16[2,16,384,1,1,128]{5,2,0,4,3,1:T(8,128)(2,1)}), bf16[2,16,384,1,1,128]{5,2,0,4,3,1:T(8,128)(2,1)}, u32[]{:S(2)}, u32[]{:S(2)}) async-start(bf16[2,16,384,1,1,128]{5,2,0,4,3,1:T(8,128)(2,1)} %copy.277), calls=%async_computation.14 | async-start | bytes 6291456 | tf_op jit(solution)/call_exported;jit(solution)/stack
  488.9 47.8 %all-to-all-start.18 = ((bf16[2,16,384,1,1,128]{5,2,0,4,3,1:T(8,128)(2,1)}), bf16[2,16,384,1,1,128]{5,2,0,4,3,1:T(8,128)(2,1)S(1)}, u32[]{:S(2)}, u32[]{:S(2)}) async-start(bf16[2,16,384,1,1,128]{5,2,0,4,3,1:T(8,128)(2,1)} %copy.286), calls=%async_computation.18 | async-start | bytes 6291456 | tf_op jit(solution)/call_exported;jit(solution)/stack
  538.4 43.8 %all-to-all-start.15 = ((bf16[2,384,8,2,1,128]{5,1,3,0,4,2:T(8,128)(2,1)}), bf16[2,384,8,2,1,128]{5,1,3,0,4,2:T(8,128)(2,1)S(1)}, u32[]{:S(2)}, u32[]{:S(2)}) async-start(bf16[2,384,8,2,1,128]{5,1,3,0,4,2:T(8,128)(2,1)} %copy.279), calls=%async_computation.15 | async-start | bytes 6291456 | tf_op jit(solution)/call_exported;jit(solution)/stack
  582.2 61.0 %all-to-all-start.19 = ((bf16[2,384,8,2,1,128]{5,1,3,0,4,2:T(8,128)(2,1)}), bf16[2,384,8,2,1,128]{5,1,3,0,4,2:T(8,128)(2,1)}, u32[]{:S(2)}, u32[]{:S(2)}) async-start(bf16[2,384,8,2,1,128]{5,1,3,0,4,2:T(8,128)(2,1)} %copy.288), calls=%async_computation.19 | async-start | bytes 6291456 | tf_op jit(solution)/call_exported;jit(solution)/stack
  (29 other events, 190.1 us)
where the time goes:
time: 660 us; the launch traced here: 650 us
  local copies, waits for them, and re-layouts  249 us (38%)
  waiting for transfers between devices  163 us (25%)
  starting transfers between devices  144 us (22%)
  other arithmetic  85.3 us (13%)
  between operations  8.91 us (1%)
    another operation x22, waiting for transfers between devices  163 us
    unnamed x88, local copies, waits for them, and re-layouts  155 us
    another operation x22, starting transfers between devices  144 us
    another operation x47, local copies, waits for them, and re-layouts  60.5 us
    convert_element_type x4, other arithmetic, quantize(): values = served.astype(jnp.float32)  27.2 us
    reduce_max x12, other arithmetic, quantize(): peak = jnp.max(jnp.abs(grouped), axis=1) + 1e-06  16.9 us
    convert_element_type x12, local copies, waits for them, and re-layouts, quantize(): values = served.astype(jnp.float32)  16.7 us
  transfers between devices with their start and end apart: 22, of which 17 were waited for; matrix products, arithmetic and copies ran while one was open for 49% of the time, Pallas kernels for 0%

commit v1 on v0

v1 whole, which is shorter than its diff:
```python
import functools

import jax
import jax.numpy as jnp
from jax import lax
from jax.experimental import pallas as pl
from jax.experimental.pallas import tpu as pltpu
from jax.sharding import PartitionSpec as P

MESH = pl.DeviceIdType.MESH
BF = jnp.bfloat16
F32 = jnp.float32
CH = 15
ROWS = 35352
LENS = (2304, 384, 384, 2304, 6144, 6144)
BASES = (0, 2304, 2688, 3072, 5376, 11520)
LAYER = 17664
SLACK = 24
Q, K, V, O, GATE, UP = range(6)


def coords():
    r, t = lax.axis_index("rep"), lax.axis_index("tp")
    return r // 4, (r // 2) % 2, r % 2, t // 4, t % 4


def dev(x, y, z, c):
    return ((x * 2 + z % 2) * 2 + c, (z // 2) * 4 + y)


def copy_wait(ref, sem):
    pltpu.make_async_copy(ref, ref, sem).wait()


def offsets(pad_ref):
    out, padding = [], jnp.int32(0)
    for l in range(2):
        for i in range(6):
            out.append(padding + (l * LAYER + BASES[i]))
            padding = padding + pad_ref[l, i]
    return out


def prep_kernel(pad_ref, flat_ref, s_out, o_out, flat, wide, s, o, in_sem, s_sem, o_sem):
    off = offsets(pad_ref)
    order = [(0, GATE), (0, UP), (1, GATE), (1, UP), (0, O), (1, O)]
    order += [(l, i) for l in range(2) for i in (Q, K, V)]

    def region(l, i):
        return l * LAYER + BASES[i], LENS[i] + SLACK

    copies = {}
    for n, (l, i) in enumerate(order):
        start, _ = region(l, i)
        size = LENS[i] + (SLACK if (l, i) == (1, UP) else 0)
        copies[(l, i)] = pltpu.make_async_copy(
            flat_ref.at[pl.ds(start, size)], flat.at[pl.ds(start, size)], in_sem.at[n])
        copies[(l, i)].start()
    for l, i in order:
        copies[(l, i)].wait()

    def widen(n, _):
        rows = pl.ds(pl.multiple_of(n * 128, 128), 128)
        wide[rows] = flat[rows].astype(F32)
        return 0

    lax.fori_loop(0, ROWS // 128, widen, 0)
    tail = pl.ds(ROWS // 128 * 128, ROWS % 128)
    wide[tail] = flat[tail].astype(F32)

    for l in range(2):
        for n, i in enumerate((GATE, UP)):
            for j in range(3):
                k = (l * 2 + n) * 3 + j
                start = off[l * 6 + i] + j

                def block(r, _):
                    rows = wide[pl.ds(start + 3 * r, 128, stride=48)]
                    s[k, r] = rows.T.astype(BF)
                    return 0

                lax.fori_loop(0, 16, block, 0)
                pltpu.make_async_copy(s.at[k], s_out.at[k], s_sem).start()
    for j in range(3):
        k = 12 + j

        def block(r, _):
            for l in range(2):
                c = 3 * r + j
                s[k, r, pl.ds(l * 64, 48)] = wide[pl.ds(off[l * 6 + Q] + c, 48, stride=48)].astype(BF)
                kk = wide[pl.ds(off[l * 6 + K] + c, 8, stride=48)]
                vv = wide[pl.ds(off[l * 6 + V] + c, 8, stride=48)]
                s[k, r, pl.ds(l * 64 + 48, 16)] = jnp.concatenate([kk, vv], axis=0).astype(BF)
            return 0

        lax.fori_loop(0, 16, block, 0)
        pltpu.make_async_copy(s.at[k], s_out.at[k], s_sem).start()

    def oblock(t, _):
        for l in range(2):
            for j in range(6):
                rows = wide[pl.ds(off[l * 6 + O] + 6 * t + j, 48, stride=48)]
                o[t, pl.ds((l * 6 + j) * 48, 48)] = rows.astype(BF)
        return 0

    lax.fori_loop(0, 8, oblock, 0)
    pltpu.make_async_copy(o, o_out, o_sem).start()
    copy_wait(s, s_sem)
    copy_wait(o, o_sem)


def prep(pads, flat):
    return pl.pallas_call(
        prep_kernel,
        out_shape=(jax.ShapeDtypeStruct((CH, 16, 128, 128), BF), jax.ShapeDtypeStruct((8, 576, 128), BF)),
        in_specs=[pl.BlockSpec(memory_space=pltpu.SMEM), pl.BlockSpec(memory_space=pl.ANY)],
        out_specs=[pl.BlockSpec(memory_space=pl.ANY)] * 2,
        scratch_shapes=[
            pltpu.VMEM((ROWS, 128), BF),
            pltpu.VMEM((ROWS, 128), F32),
            pltpu.VMEM((CH, 16, 128, 128), BF),
            pltpu.VMEM((8, 576, 128), BF),
            pltpu.SemaphoreType.DMA((12,)),
            pltpu.SemaphoreType.DMA,
            pltpu.SemaphoreType.DMA,
        ],
        compiler_params=pltpu.CompilerParams(vmem_limit_bytes=60 * 2**20),
    )(pads, flat)


def exchange_kernel(s, o, f, fo, r1, r2, xs, xr, zs, zr, ys, yr, os, orr):
    x, zl, c, zh, y = coords()
    z = zh * 2 + zl
    partners = [dev((x + j) % 4, y, z, c) for j in (1, 2, 3)]
    partners += [dev(x, (y + j) % 4, z, c) for j in (1, 2, 3)]
    partners += [dev(x, y, (z + i // 2) % 4, (c + i % 2) % 2) for i in range(1, 8)]
    partners += [dev(x, (y + i) % 4, (z + 2) % 4, c) for i in range(4)]
    barrier = pltpu.get_barrier_semaphore()
    for d in partners:
        pl.semaphore_signal(barrier, inc=1, device_id=d, device_id_type=MESH)
    pl.semaphore_wait(barrier, len(partners))

    def remote(src, dst, send, recv, d):
        pltpu.make_async_remote_copy(
            src_ref=src, dst_ref=dst, send_sem=send, recv_sem=recv, device_id=d, device_id_type=MESH).start()

    def send_x(k):
        for j in (1, 3, 2):
            xd = (x + j) % 4
            remote(s.at[k, xd], r1.at[k, x], xs, xr.at[k], dev(xd, y, z, c))
        pltpu.make_async_copy(s.at[k, x], r1.at[k, x], xr.at[k]).start()

    def send_z(k):
        for i in (2, 6, 4, 3, 7, 5, 1):
            zd, cd = (z + i // 2) % 4, (c + i % 2) % 2
            remote(r1.at[k, pl.ds(zd // 2 * 2, 2), zd % 2, cd], r2.at[k, :, zl, zh, c], zs, zr.at[k], dev(x, y, zd, cd))
        pltpu.make_async_copy(r1.at[k, pl.ds(zh * 2, 2), zl, c], r2.at[k, :, zl, zh, c], zr.at[k]).start()

    def send_y(k):
        for j in (1, 3, 2):
            yd = (y + j) % 4
            remote(r2.at[k, yd // 2, yd % 2], f.at[k, y], ys, yr, dev(x, yd, z, c))
        pltpu.make_async_copy(r2.at[k, y // 2, y % 2], f.at[k, y], yr).start()

    for i in (1, 3, 2, 5, 7, 6, 4):
        yd, zhd = (y + i % 4) % 4, (zh + i // 4) % 2
        remote(o.at[zhd * 4 + yd], fo.at[zh * 4 + y], os, orr, dev(x, yd, zhd * 2 + zl, c))
    pltpu.make_async_copy(o.at[zh * 4 + y], fo.at[zh * 4 + y], orr).start()

    def first(k, _):
        send_x(k)
        return 0

    lax.fori_loop(0, CH, first, 0)

    def step(k, _):
        copy_wait(r1.at[k], xr.at[k])
        send_z(k)

        @pl.when(k > 0)
        def _():
            copy_wait(r2.at[k - 1], zr.at[k - 1])
            send_y(k - 1)

        return 0

    lax.fori_loop(0, CH, step, 0)
    copy_wait(r2.at[CH - 1], zr.at[CH - 1])
    send_y(CH - 1)
    copy_wait(f, yr)
    copy_wait(fo, orr)
    copy_wait(s.at[:, pl.ds(0, 3)], xs)
    copy_wait(s.at[:, pl.ds(0, 3)], ys)
    copy_wait(s.at[:, pl.ds(0, 3)], zs)
    copy_wait(s.at[:, 0, 0], zs)
    copy_wait(fo.at[pl.ds(0, 7)], os)


def exchange(s, o):
    dma = pltpu.SemaphoreType.DMA
    return pl.pallas_call(
        exchange_kernel,
        out_shape=(jax.ShapeDtypeStruct((CH, 4, 2, 2, 128, 128), BF), jax.ShapeDtypeStruct((8, 576, 128), BF)),
        in_specs=[pl.BlockSpec(memory_space=pl.ANY)] * 2,
        out_specs=[pl.BlockSpec(memory_space=pl.ANY)] * 2,
        scratch_shapes=[
            pltpu.VMEM((CH, 4, 2, 2, 128, 128), BF),
            pltpu.VMEM((CH, 2, 2, 2, 2, 128, 128), BF),
            dma, dma((CH,)), dma, dma((CH,)), dma, dma, dma, dma,
        ],
        compiler_params=pltpu.CompilerParams(
            collective_id=0, has_side_effects=True, vmem_limit_bytes=60 * 2**20),
    )(s, o)


def quantize(values):
    peak = jnp.max(jnp.abs(values), axis=0, keepdims=True) + 1e-6
    return (values * (1.0 / peak)).astype(BF), peak


def finish_kernel(f_ref, fo_ref, q, qs, k, ks, v, vs, o, os, gate, gs, up, us,
                  f, fo, qb, kb, vb, ob, gb, in_sem, o_sem, out_sem):
    for n in range(CH):
        pltpu.make_async_copy(f_ref.at[n], f.at[n], in_sem.at[n]).start()
    pltpu.make_async_copy(fo_ref, fo, o_sem).start()

    def put(src, dst, n):
        pltpu.make_async_copy(src, dst, out_sem.at[n]).start()

    for n in range(12):
        copy_wait(f.at[n], in_sem.at[n])
        l, which, j = n // 6, n // 3 % 2, n % 3
        scale = (gs, us)[which]
        for src in range(16):
            c, zh, y = src // 8, src // 4 % 2, src % 4
            cols = pl.ds(src * 128, 128)
            scaled, peak = quantize(f[n, y, zh, c].astype(F32))
            gb[n, :, cols] = scaled
            scale[j, pl.ds(l, 1), cols] = peak
        put(gb.at[n], (gate, up)[which].at[l, pl.ds(j * 128, 128)], 0)
    sources = [(s % 4, s // 4 % 2, s // 8) for s in range(16)]
    for j in range(3):
        n = 12 + j
        copy_wait(f.at[n], in_sem.at[n])
        for l in range(2):
            base = l * 64
            rows = [f[n, y, zh, c, pl.ds(base, 48)].astype(F32) for y, zh, c in sources]
            qb[l, j], qs[j, pl.ds(l, 1)] = quantize(jnp.concatenate(rows, axis=0).T)
            both = [f[n, y, zh, c, pl.ds(base + 48, 16)].astype(F32) for y, zh, c in sources]
            kb[l, j], ks[j, pl.ds(l, 1)] = quantize(jnp.concatenate([b[:8] for b in both], axis=0).T)
            vb[l, j], vs[j, pl.ds(l, 1)] = quantize(jnp.concatenate([b[8:] for b in both], axis=0).T)
            rows = pl.ds(j * 128, 128)
            put(qb.at[l, j], q.at[l, rows], 1)
            put(kb.at[l, j], k.at[l, rows], 2)
            put(vb.at[l, j], v.at[l, rows], 3)
    copy_wait(fo, o_sem)
    for l in range(2):
        for j in range(6):
            rows = [fo[t, pl.ds((l * 6 + j) * 48, 48)].astype(F32) for t in range(8)]
            ob[l, j], os[j, pl.ds(l, 1)] = quantize(jnp.concatenate(rows, axis=0).T)
            put(ob.at[l, j], o.at[l, pl.ds(j * 128, 128)], 4)
    for n, buffer in enumerate((gb, qb, kb, vb, ob)):
        copy_wait(buffer, out_sem.at[n])


def finish(f, fo):
    shapes = [((2, 384, 768), (3, 2, 768)), ((2, 384, 128), (3, 2, 128)), ((2, 384, 128), (3, 2, 128)),
              ((2, 768, 384), (6, 2, 384)), ((2, 384, 2048), (3, 2, 2048)), ((2, 384, 2048), (3, 2, 2048))]
    out_shape, out_specs = [], []
    for served, scale in shapes:
        out_shape += [jax.ShapeDtypeStruct(served, BF), jax.ShapeDtypeStruct(scale, F32)]
        out_specs += [pl.BlockSpec(memory_space=pl.ANY), pl.BlockSpec(memory_space=pltpu.VMEM)]
    dma = pltpu.SemaphoreType.DMA
    return pl.pallas_call(
        finish_kernel,
        out_shape=out_shape,
        in_specs=[pl.BlockSpec(memory_space=pl.ANY)] * 2,
        out_specs=out_specs,
        scratch_shapes=[
            pltpu.VMEM((CH, 4, 2, 2, 128, 128), BF),
            pltpu.VMEM((8, 576, 128), BF),
            pltpu.VMEM((2, 3, 128, 768), BF),
            pltpu.VMEM((2, 3, 128, 128), BF),
            pltpu.VMEM((2, 3, 128, 128), BF),
            pltpu.VMEM((2, 6, 128, 384), BF),
            pltpu.VMEM((12, 128, 2048), BF),
            dma((CH,)), dma, dma((5,)),
        ],
        compiler_params=pltpu.CompilerParams(vmem_limit_bytes=60 * 2**20),
    )(f, fo)


def local(flat, pads):
    s, o = prep(pads, flat.reshape(ROWS, 128))
    f, fo = exchange(s.reshape(CH, 4, 2, 2, 128, 128), o)
    outs = finish(f, fo)
    return tuple(a.transpose(1, 0, 2) if n % 2 else a for n, a in enumerate(outs))


def solution(mesh):
    a, b = P(None, "rep", "tp"), P(None, "tp", "rep")
    specs = (a, a, a, a, a, a, b, b, a, a, a, a)
    return jax.shard_map(
        local, mesh=mesh, in_specs=(P(("rep", "tp")), P()), out_specs=specs, check_vma=False)
```

time: 660 us -> 158 us (0.24)
  the two profiles are of different devices: /device:TPU:96 before, /device:TPU:1 now
where the time goes in v1:
time: 158 us
  Pallas kernels  157 us (99%)
    pallas_call x1, Pallas kernels, exchange(): pl.pallas_call(exchange_kernel, out_shape=(jax.ShapeDtypeStruct((CH, 4, 2...  119 us
    pallas_call x1, Pallas kernels, prep(): pl.pallas_call(prep_kernel, out_shape=(jax.ShapeDtypeStruct((CH, 16, 128,...  30.4 us
    pallas_call x1, Pallas kernels, finish(): pl.pallas_call(finish_kernel, out_shape=out_shape, in_specs=[pl.BlockSpec...  7.89 us

profile of v1, /device:TPU:1, one launch (start us, length us, event | category | flops | bytes accessed | tf_op | source)
XLA Modules:
  0.0 157.8 jit_solution(824755678606398915)
XLA Ops:
  0.6 30.4 %shard_map.121 = (bf16[15,16,128,128]{3,2,1,0:T(8,128)(2,1)}, bf16[8,576,128]{2,1,0:T(8,128)(2,1)}) custom-call(s32[2,6]{1,0:T(2,128)} %pad_ref.1, bf16[35352,128]{1,0:T(8,128)(2,1)} %bitcast.8), custom_call_target="tpu_custom_call" | custom-call | tf_op jit(solution)/shard_map/pallas_call | solution.py:113
  31.1 118.8 %shard_map.122 = (bf16[15,4,2,2,128,128]{5,4,3,2,1,0:T(8,128)(2,1)}, bf16[8,576,128]{2,1,0:T(8,128)(2,1)}) custom-call(bf16[15,4,2,2,128,128]{5,4,3,2,1,0:T(8,128)(2,1)} %bitcast.9, bf16[8,576,128]{2,1,0:T(8,128)(2,1)} %get-tuple-element.29.o), custom_call_target="tpu_custom_call" | custom-call | tf_op jit(solution)/shard_map/pallas_call | solution.py:201
  149.9 7.9 %shard_map.123 = (bf16[2,384,768]{2,1,0:T(8,128)(2,1)}, f32[3,2,768]{2,1,0:T(2,128)}, bf16[2,384,128]{2,1,0:T(8,128)(2,1)}, f32[3,2,128]{2,1,0:T(2,128)}, bf16[2...) custom-call(bf16[15,4,2,2,128,128]{5,4,3,2,1,0:T(8,128)(2,1)} %get-t, ...), custom_call_target="tpu_custom_call" | custom-call | tf_op jit(solution)/shard_map/pallas_call | solution.py:274
